TPU v7x, 256 devices: a whole 4x4x8 slice. The times are simulated.
256 devices in a mesh: batch: 16 (over y, x), field: 2 (over core), dim: 8 (over z).
Axes of the slice: x: 4, y: 4, z: 8, core: 2. Of those that a mesh axis runs over, the one named last changes fastest.
Arguments:
- features: bfloat16 [26, 128, 16384], P('field', 'dim', 'batch'), may hold values from -6 to 6
- cross_weight: bfloat16 [2, 26, 128, 26, 128], P(None, 'field', 'dim'), may hold values from -0.109375 to 0.109375
- cross_bias: float32 [2, 26, 128], P(None, 'field', 'dim'), may hold values from -3 to 3
- tower_weight: bfloat16 [1024, 26, 128], P(('field', 'dim')), may hold values from -0.109375 to 0.109375
- tower_bias: float32 [1024], P(('field', 'dim')), may hold values from -3 to 3
- query_weight: bfloat16 [1024, 128], P(('field', 'dim')), may hold values from -0.1875 to 0.1875
- user_vec: bfloat16 [16384, 128], P('batch'), may hold values from -6 to 6
- candidates: bfloat16 [4096, 128], P('batch'), may hold values from -6 to 6
- positive: int32 [16384], P('batch'), may hold values from 0 to 4095
Outputs:
- crossed: bfloat16 [26, 128, 16384], P('field', 'dim', 'batch')
- losses: float32 [16384], P('batch')
All inputs are finite; a program needn't handle non-finite values.
Results may differ from a plain program's by a relative error of at most 0.0049.
Values may be sent and summed in bfloat16 or wider, within the bound.
A program may use at most 64 MiB of HBM per device.

v0:
```python
import math
import jax
import jax.numpy as jnp
from jax import lax
from jax.sharding import Mesh
from jax.sharding import PartitionSpec as P

CROSS = 2
BATCH = ("batch_0", "batch_1")


def whole_of(x, axes, dim):
    if not axes:
        return x
    nearer = lax.all_gather(x, axes[-1], axis=dim, tiled=True)
    return whole_of(nearer, axes[:-1], dim)


def cut_along(x, dim, length):
    shape = x.shape
    pieces = x.reshape(*shape[:dim], length, shape[dim] // length, *shape[dim + 1 :])
    return jnp.moveaxis(pieces, dim, 0)


def summed_on_arrival(x, axis, dim):
    length = lax.axis_size(axis)
    pieces = lax.all_to_all(cut_along(x, dim, length), axis, 0, 0, tiled=True)
    return jnp.sum(pieces.astype(jnp.float32), axis=0)


def laid_out(pieces, dim):
    shape = list(pieces.shape[1:])
    shape[dim] *= pieces.shape[0]
    return jnp.moveaxis(pieces, 0, dim).reshape(shape)


def sent_to_all(x, axis):
    copies = jnp.broadcast_to(x, (lax.axis_size(axis), *x.shape))
    return lax.all_to_all(copies, axis, split_axis=0, concat_axis=0, tiled=True)


def gather_directly(x, axis, dim):
    return laid_out(sent_to_all(x, axis), dim)


def by_device(weights, field_count, dim_count):
    out_count, fields_all, entries_all = weights.shape
    shaped = weights.reshape(
        out_count, field_count, fields_all // field_count, dim_count, entries_all // dim_count
    )
    shaped = shaped.transpose(1, 3, 0, 2, 4)
    return shaped.reshape(
        field_count * dim_count, out_count, fields_all // field_count * (entries_all // dim_count)
    )


def row_adder(blocks, shards):
    return jnp.einsum("kib,koi->ob", shards, blocks, preferred_element_type=jnp.float32)


def cross_flat(current, blocks):
    field_local, entry_local, row_count = current.shape
    flattened = current.reshape(1, field_local * entry_local, row_count)
    return row_adder(blocks, lax.all_gather(flattened, ("field", "dim"), axis=0, tiled=True))


def next_layer(anchor, current, product, bias_vec):
    field_local, entry_local, row_count = current.shape
    gated = (product + bias_vec.reshape(field_local * entry_local, 1)).reshape(
        field_local, entry_local, row_count
    )
    return (anchor * gated + current.astype(jnp.float32)).astype(jnp.bfloat16)


def candidate_loss(query_vec, targets, candidates):
    score_scale = 1.0 / math.sqrt(query_vec.shape[1])
    row_count = query_vec.shape[0]
    running_max = jnp.full((row_count,), -1e30, jnp.float32)
    logits = (
        jnp.einsum(
            "be,ce->bc",
            query_vec,
            whole_of(candidates, BATCH, 0),
            preferred_element_type=jnp.float32,
        )
        * score_scale
    )
    labels = lax.broadcasted_iota(jnp.int32, logits.shape, 1)
    picked = jnp.sum(jnp.where(labels == targets[:, None], logits, 0.0), axis=1)
    new_max = jnp.maximum(running_max, jnp.max(logits, axis=1))
    running_sum = jnp.sum(jnp.exp(logits - new_max[:, None]), axis=1)
    best_score, exp_total, picked = (new_max, running_sum, picked)
    return best_score + jnp.log(exp_total) - picked


def body(
    features,
    cross_weight,
    cross_bias,
    tower_weight,
    tower_bias,
    query_weight,
    user_vec,
    candidates,
    positive,
):
    field_count = lax.axis_size("field")
    dim_count = lax.axis_size("dim")
    field_local, entry_local, row_count = features.shape
    column_count = field_local * entry_local
    anchor = features.astype(jnp.float32)
    current = features
    stacked = cross_weight.reshape(
        CROSS, column_count, cross_weight.shape[3], cross_weight.shape[4]
    )
    for level_idx in range(CROSS):
        blocks = by_device(stacked[level_idx], field_count, dim_count)
        product = cross_flat(current, blocks)
        current = next_layer(anchor, current, product, cross_bias[level_idx])
    tower_blocks = by_device(tower_weight, field_count, dim_count)
    flattened = current.reshape(1, column_count, row_count)
    tower_pre = row_adder(
        tower_blocks, lax.all_gather(flattened, ("field", "dim"), axis=0, tiled=True)
    )
    hidden = jax.nn.relu(tower_pre + tower_bias[:, None]).astype(jnp.bfloat16)
    partial_value = lax.dot_general(
        hidden, query_weight, (((0,), (0,)), ((), ())), preferred_element_type=jnp.float32
    )
    share_rows = row_count // (field_count * dim_count)
    member = lax.axis_index(("field", "dim"))
    query_part = summed_on_arrival(partial_value.astype(jnp.bfloat16), ("field", "dim"), 0)
    user_rows = lax.dynamic_slice_in_dim(user_vec, member * share_rows, share_rows, 0)
    targets = lax.dynamic_slice_in_dim(positive, member * share_rows, share_rows, 0)
    query_vec = (query_part + user_rows.astype(jnp.float32)).astype(jnp.bfloat16)
    part_loss = candidate_loss(query_vec, targets, candidates)
    losses = gather_directly(part_loss, ("field", "dim"), 0)
    return (current, losses)


def solution(mesh):
    torus = Mesh(
        mesh.devices.reshape(4, 4, mesh.shape["field"], mesh.shape["dim"]),
        ("batch_0", "batch_1", "field", "dim"),
    )
    in_specs = (
        P("field", "dim", BATCH),
        P(None, "field", "dim", None, None),
        P(None, "field", "dim"),
        P(("field", "dim"), None, None),
        P(("field", "dim")),
        P(("field", "dim"), None),
        P(BATCH, None),
        P(BATCH, None),
        P(BATCH),
    )
    out_specs = (P("field", "dim", BATCH), P(BATCH))
    return jax.shard_map(body, mesh=torus, in_specs=in_specs, out_specs=out_specs, check_vma=False)
```

profile of v0, /device:TPU:1, one launch (start us, length us, event | category | flops | bytes accessed | tf_op | source)
XLA Modules:
  0.0 219.8 jit_solution(14988092904554589448)
XLA Ops:
  7.2 0.0 copy-start
  7.2 0.0 all-gather.5.cloned.1.call-start
  7.2 0.7 all-gather.5.cloned.1.call-update
  7.9 0.0 all-gather.7.cloned.1.call-start
  8.0 2.2 %fusion.13 = (bf16[1,13,16,26,128]{4,2,3,1,0:T(8,128)(2,1)S(1)}, bf16[1,13,16,26,128]{4,2,3,1,0:T(8,128)(2,1)S(1)}) fusion(bf16[2,13,16,26,128]{4,2,3,1,0:T(8,128)(2,1)} %param.10), kind=kLoop, calls=%fused_computation.29 | loop fusion | bytes 5537792 | tf_op jit(solution)/shard_map/slice | solution.py:117
  10.2 0.2 copy.19
  10.4 8.7 %reshape_squeeze.8 = bf16[208,2,13,8,16]{4,3,0,2,1:T(8,128)(2,1)} reshape(bf16[1,13,16,26,128]{4,2,1,3,0:T(8,128)(2,1)S(1)} %copy.19) | data formatting | bytes 2768896 | tf_op jit(solution)/shard_map/reshape;squeeze | solution.py:48
  19.1 10.9 %copy.20 = bf16[2,8,208,13,16]{2,4,3,1,0:T(8,128)(2,1)S(1)} copy(bf16[2,8,208,13,16]{4,1,2,3,0:T(8,128)(2,1)} %bitcast.50) | data formatting | bytes 2768896 | tf_op jit(solution)/shard_map/transpose | solution.py:51
  30.1 0.0 copy-done.5
  30.1 0.1 add.51
  30.2 32.3 %all-gather.5.cloned.1.call-done = bf16[16,208,1024]{2,1,0:T(8,128)(2,1)} async-done(((bf16[1,208,1024]{2,1,0:T(8,128)(2,1)}), bf16[16,208,1024]{2,1,0:T(8,128)(2,1)}) %all-gather.5.cloned.1.call-update) | async-done | bytes 6815760 | tf_op jit(solution)/shard_map/all_gather | solution.py:64
  62.5 4.6 %fusion = f32[208,1024]{1,0:T(8,128)S(1)} fusion(bf16[16,208,208]{1,2,0:T(8,128)(2,1)S(1)} %bitcast.52, bf16[16,208,1024]{2,1,0:T(8,128)(2,1)} %all-gather.5.cloned.1.call-done, f32[208]{0:T(256)S(1)} %add.51), kind=kOutput, calls=%fused_computation.4 | convolution fusion | flops 1417887744 | bytes 9052992 | tf_op jit(solution)/shard_map/kib,koi->ob/dot_general | solution.py:58
  67.1 0.0 copy-done.1
  67.1 0.9 fusion.7
  68.0 0.0 all-gather.7.cloned.1.call-update
  68.0 0.0 all-gather.9.cloned.1.call-start
  68.1 0.2 copy.22
  68.3 8.7 %reshape_squeeze.9 = bf16[208,2,13,8,16]{4,3,0,2,1:T(8,128)(2,1)} reshape(bf16[1,13,16,26,128]{4,2,1,3,0:T(8,128)(2,1)S(1)} %copy.22) | data formatting | bytes 2768896 | tf_op jit(solution)/shard_map/reshape;squeeze | solution.py:48
  77.0 11.2 %copy.23 = bf16[2,8,208,13,16]{2,4,3,1,0:T(8,128)(2,1)S(1)} copy(bf16[2,8,208,13,16]{4,1,2,3,0:T(8,128)(2,1)} %bitcast.51) | data formatting | bytes 2768896 | tf_op jit(solution)/shard_map/transpose | solution.py:51
  88.2 0.1 add.55
  88.2 26.9 %all-gather.7.cloned.1.call-done = bf16[16,208,1024]{2,1,0:T(8,128)(2,1)} async-done(((bf16[1,208,1024]{2,1,0:T(8,128)(2,1)}), bf16[16,208,1024]{2,1,0:T(8,128)(2,1)}) %all-gather.7.cloned.1.call-update) | async-done | bytes 6815760 | tf_op jit(solution)/shard_map/all_gather | solution.py:64
  115.2 4.6 %fusion.1 = f32[1024,208]{0,1:T(8,128)S(1)} fusion(bf16[16,208,1024]{2,1,0:T(8,128)(2,1)} %all-gather.7.cloned.1.call-done, bf16[16,208,208]{1,2,0:T(8,128)(2,1)S(1)} %bitcast.58, f32[208]{0:T(256)S(1)} %add.55), kind=kOutput, calls=%fused_computation.5 | convolution fusion | flops 1417887744 | bytes 9052992 | tf_op jit(solution)/shard_map/kib,koi->ob/dot_general | solution.py:58
  119.8 0.0 copy-start.3
  119.8 0.0 copy-done.2
  119.8 0.0 copy-start.6
  119.9 1.0 fusion.6
  120.8 0.0 all-gather.9.cloned.1.call-update
  120.8 0.0 all-gather.11.cloned.1.call-start
  120.9 0.0 copy-done.4
  120.9 10.4 %all_gather.18 = bf16[1024,128]{1,0:T(8,128)(2,1)} all-gather(bf16[256,128]{1,0:T(8,128)(2,1)S(1)} %copy-done.4), channel_id=1, replica_groups=mesh['batch_0'=4,'batch_1'=4,'field'=2,'dim'=8] {'batch_1'}, dimensions={0}, use_global_device_ids=true | all-gather | bytes 327680 | tf_op jit(solution)/shard_map/all_gather | solution.py:15
  131.3 0.0 all-gather.11.cloned.1.call-update
  131.4 0.0 copy-done.3
  131.4 0.4 copy.25
  131.8 0.1 copy.26
  132.0 36.0 %all-gather.9.cloned.1.call-done = bf16[16,208,1024]{2,1,0:T(8,128)(2,1)} async-done(((bf16[1,208,1024]{2,1,0:T(8,128)(2,1)}), bf16[16,208,1024]{2,1,0:T(8,128)(2,1)}) %all-gather.9.cloned.1.call-update) | async-done | bytes 6815760 | tf_op jit(solution)/shard_map/all_gather | solution.py:123
  168.0 0.0 copy-done
  168.0 0.0 copy-done.6
  168.0 5.3 %convolution_convert_fusion = bf16[1024,128]{1,0:T(8,128)(2,1)} fusion(bf16[64,128]{1,0:T(8,128)(2,1)S(1)} %copy-done, bf16[16,208,1024]{2,1,0:T(8,128)(2,1)} %all-gather.9.cloned.1.call-done, bf16[16,64,208]{1,2,0:T(8,128)(2,1)S(1)} %bitcast.56, f32[64]{0:T(128)S(1)} %copy-done.6), kind=kOutput, calls=%fused_computation.6 | convolution fusion | flops 453312512 | bytes 7520512 | tf_op jit(solution)/shard_map/dot_general | solution.py:126
  173.3 4.6 %all-to-all-start = ((bf16[16,64,128]{2,1,0:T(8,128)(2,1)}), bf16[16,64,128]{2,1,0:T(8,128)(2,1)S(1)}, u32[]{:S(2)}, u32[]{:S(2)}) async-start(bf16[16,64,128]{2,1,0:T(8,128)(2,1)} %bitcast.16), calls=%async_computation | async-start | bytes 524288 | tf_op jit(solution)/shard_map/all_to_all | solution.py:27
  177.9 0.8 dynamic_slice.7
  178.6 8.9 %all-to-all-done = bf16[16,64,128]{2,1,0:T(8,128)(2,1)S(1)} async-done(((bf16[16,64,128]{2,1,0:T(8,128)(2,1)}), bf16[16,64,128]{2,1,0:T(8,128)(2,1)S(1)}, u32[]{:S(2)}, u32[]{:S(2)}) %all-to-all-start) | async-done | bytes 262176 | tf_op jit(solution)/shard_map/all_to_all | solution.py:27
  187.5 4.9 %all-gather.11.cloned.1.call-done = bf16[4096,128]{1,0:T(8,128)(2,1)} async-done(((bf16[1024,128]{1,0:T(8,128)(2,1)}), bf16[4096,128]{1,0:T(8,128)(2,1)}) %all-gather.11.cloned.1.call-update) | async-done | bytes 1048592 | tf_op jit(solution)/shard_map/all_gather | solution.py:15
  192.5 1.8 fusion.14
  194.3 0.5 exponential_reduce_fusion
  194.8 16.6 %all_to_all.11 = f32[16,1,64]{2,1,0:T(1,128)S(1)} all-to-all(f32[16,1,64]{2,1,0:T(1,128)S(1)} %broadcast_in_dim.15), channel_id=1, replica_groups=mesh['batch_0'=4,'batch_1'=4,'field'=2,'dim'=8] {'field','dim'}, dimensions={0} | all-to-all | bytes 8192 | tf_op jit(solution)/shard_map/all_to_all | solution.py:39
  211.4 0.5 broadcast.18
  211.9 0.7 reduce.7
  212.6 0.7 reshape.64
  (9 shorter events, 0.1 us)
Async XLA Ops:
  7.2 160.8 %copy-start = (bf16[64,128]{1,0:T(8,128)(2,1)S(1)}, bf16[64,128]{1,0:T(8,128)(2,1)}, u32[]{:S(2)}) copy-start(bf16[64,128]{1,0:T(8,128)(2,1)} %param.14) | copy-start | bytes 49156
  7.2 55.3 %all-gather.5.cloned.1.call-start = ((), (), s32[]{:S(2)}) async-start(), calls=%async_computation.2 | async-start | bytes 7241728 | tf_op jit(solution)/shard_map/all_gather | solution.py:64
  7.9 107.3 %all-gather.7.cloned.1.call-start = ((), (), s32[]{:S(2)}) async-start(), calls=%async_computation.3 | async-start | bytes 7241728 | tf_op jit(solution)/shard_map/all_gather | solution.py:64
  19.1 11.0 %copy-start.5 = (f32[2,13,16]{2,0,1:T(2,128)S(1)}, f32[2,13,16]{2,0,1:T(2,128)}, u32[]{:S(2)}) copy-start(f32[2,13,16]{2,0,1:T(2,128)} %param.11) | copy-start | bytes 4996
  62.5 4.6 %copy-start.1 = (bf16[13,16,1024]{2,1,0:T(8,128)(2,1)S(1)}, bf16[13,16,1024]{2,1,0:T(8,128)(2,1)}, u32[]{:S(2)}) copy-start(bf16[13,16,1024]{2,1,0:T(8,128)(2,1)} %param.9) | copy-start | bytes 1277956
  68.0 100.0 %all-gather.9.cloned.1.call-start = ((), (), s32[]{:S(2)}) async-start(), calls=%async_computation.4 | async-start | bytes 7241728 | tf_op jit(solution)/shard_map/all_gather | solution.py:123
  115.2 4.7 %copy-start.2 = (bf16[13,16,1024]{2,1,0:T(8,128)(2,1)S(1)}, bf16[13,16,1024]{2,1,0:T(8,128)(2,1)}, u32[]{:S(2)}) copy-start(bf16[13,16,1024]{2,1,0:T(8,128)(2,1)} %fusion.7) | copy-start | bytes 1277956
  115.2 5.7 %copy-start.4 = (bf16[256,128]{1,0:T(8,128)(2,1)S(1)}, bf16[256,128]{1,0:T(8,128)(2,1)}, u32[]{:S(2)}) copy-start(bf16[256,128]{1,0:T(8,128)(2,1)} %param.16) | copy-start | bytes 196612
  119.8 11.6 %copy-start.3 = (bf16[64,26,128]{2,0,1:T(8,128)(2,1)S(1)}, bf16[64,26,128]{2,0,1:T(8,128)(2,1)}, u32[]{:S(2)}) copy-start(bf16[64,26,128]{2,0,1:T(8,128)(2,1)} %param.12) | copy-start | bytes 1277956
  119.8 48.2 %copy-start.6 = (f32[64]{0:T(128)S(1)}, f32[64]{0:T(128)}, u32[]{:S(2)}) copy-start(f32[64]{0:T(128)} %param.13) | copy-start | bytes 772
  120.8 71.6 %all-gather.11.cloned.1.call-start = ((), (), s32[]{:S(2)}) async-start(), calls=%async_computation.5 | async-start | bytes 1310720 | tf_op jit(solution)/shard_map/all_gather | solution.py:15
  173.3 14.2 %all-to-all-start = ((bf16[16,64,128]{2,1,0:T(8,128)(2,1)}), bf16[16,64,128]{2,1,0:T(8,128)(2,1)S(1)}, u32[]{:S(2)}, u32[]{:S(2)}) async-start(bf16[16,64,128]{2,1,0:T(8,128)(2,1)} %bitcast.16), calls=%async_computation | async-start | bytes 524288 | tf_op jit(solution)/shard_map/all_to_all | solution.py:27
Sparse Core Ops, SparseCore 0:
  9.8 52.6 all-gather.4
  68.1 46.9 all-gather.6
  121.0 46.9 all-gather.8
  169.7 22.7 all-gather.10
where the time goes:
time: 220 us
  waiting for transfers between devices  110 us (50%)
  local copies, waits for them, and re-layouts  44.9 us (20%)
  blocking collectives  27 us (12%)
  matrix products  16.3 us (7%)
  between operations  13.9 us (6%)
  starting transfers between devices  4.74 us (2%)
  other arithmetic  3.03 us (1%)
    all_gather x2, waiting for transfers between devices, cross_flat(): lax.all_gather(flattened, ('field', 'dim'), axis=0, tiled=True)  59.2 us
    all_gather x1, waiting for transfers between devices, body(): lax.all_gather(flattened, ('field', 'dim'), axis=0, tiled=True)  36 us
    transpose x3, local copies, waits for them, and re-layouts, by_device(): shaped = shaped.transpose(1, 3, 0, 2, 4)  22.3 us
    another operation x2, local copies, waits for them, and re-layouts, by_device(): weights.reshape(out_count, field_count, fields_all // field_count, dim_co...  17.4 us
    all_to_all x1, blocking collectives, sent_to_all(): return lax.all_to_all(copies, axis, split_axis=0, concat_axis=0, tiled=True)  16.6 us
    all_gather x1, blocking collectives, whole_of(): nearer = lax.all_gather(x, axes[-1], axis=dim, tiled=True)  10.4 us
    dot_general x2, matrix products, row_adder(): jnp.einsum('kib,koi->ob', shards, blocks, preferred_element_type=jnp.floa...  9.24 us
    all_to_all x1, waiting for transfers between devices, summed_on_arrival(): pieces = lax.all_to_all(cut_along(x, dim, length), axis, 0, 0, tiled=True)  8.89 us
  transfers between devices with their start and end apart: 5, of which 5 were waited for; matrix products, arithmetic and copies ran while one was open for 22% of the time, Pallas kernels for 0%

commit v1 on v0

--- a/solution.py
+++ b/solution.py
@@ -120,7 +120,13 @@
     tower_blocks = by_device(tower_weight, field_count, dim_count)
     flattened = current.reshape(1, column_count, row_count)
     tower_pre = row_adder(
-        tower_blocks, lax.all_gather(flattened, ("field", "dim"), axis=0, tiled=True)
+        tower_blocks,
+        jnp.concatenate(
+            lax.all_to_all(
+                jnp.stack([flattened] * lax.axis_size(("field", "dim"))), ("field", "dim"), 0, 0
+            ),
+            axis=0,
+        ),
     )
     hidden = jax.nn.relu(tower_pre + tower_bias[:, None]).astype(jnp.bfloat16)
     partial_value = lax.dot_general(

time: 220 us -> 324 us (1.47)
  waiting for transfers between devices: 110 us -> 206 us
  starting transfers between devices: 4.74 us -> 11.7 us
  blocking collectives: 27 us -> 22.9 us
  local copies, waits for them, and re-layouts: 44.9 us -> 48.7 us
    all_to_all x0 -> x1, waiting for transfers between devices: none -> 137 us  [body(): lax.all_to_all(jnp.stack([flattened] * lax.axis_size(('field', 'dim'))),...]
    all_gather x1 -> x0, waiting for transfers between devices: 36 us -> none  [body(): lax.all_gather(flattened, ('field', 'dim'), axis=0, tiled=True)]
    all_gather x1, waiting for transfers between devices: 4.93 us -> 0.03 us  [whole_of(): nearer = lax.all_gather(x, axes[-1], axis=dim, tiled=True)]
    all_to_all x0 -> x1, starting transfers between devices: none -> 4.87 us  [body(): lax.all_to_all(jnp.stack([flattened] * lax.axis_size(('field', 'dim'))),...]
    all_to_all x1, blocking collectives: 16.6 us -> 11.7 us  [sent_to_all(): return lax.all_to_all(copies, axis, split_axis=0, concat_axis=0, tiled=True)]
    another operation x0 -> x1, local copies, waits for them, and re-layouts: none -> 3.72 us  [body(): jnp.stack([flattened] * lax.axis_size(('field', 'dim')))]
  transfers between devices with their start and end apart: 5 -> 5, of which waited for: 5 -> 4; matrix products, arithmetic and copies ran while one was open for 22% -> 15% of each run, Pallas kernels for 0% -> 0%
where the time goes in v1:
time: 324 us; the launch traced here: 323 us
  waiting for transfers between devices  206 us (64%)
  local copies, waits for them, and re-layouts  48.7 us (15%)
  blocking collectives  22.9 us (7%)
  matrix products  16.3 us (5%)
  between operations  15.7 us (5%)
  starting transfers between devices  11.7 us (4%)
    all_to_all x1, waiting for transfers between devices, body(): lax.all_to_all(jnp.stack([flattened] * lax.axis_size(('field', 'dim'))),...  137 us
    all_gather x2, waiting for transfers between devices, cross_flat(): lax.all_gather(flattened, ('field', 'dim'), axis=0, tiled=True)  59.2 us
    transpose x3, local copies, waits for them, and re-layouts, by_device(): shaped = shaped.transpose(1, 3, 0, 2, 4)  22.3 us
    another operation x2, local copies, waits for them, and re-layouts, by_device(): weights.reshape(out_count, field_count, fields_all // field_count, dim_co...  17.4 us
    all_to_all x1, blocking collectives, sent_to_all(): return lax.all_to_all(copies, axis, split_axis=0, concat_axis=0, tiled=True)  11.7 us
    all_gather x1, blocking collectives, whole_of(): nearer = lax.all_gather(x, axes[-1], axis=dim, tiled=True)  11.1 us
    dot_general x2, matrix products, row_adder(): jnp.einsum('kib,koi->ob', shards, blocks, preferred_element_type=jnp.floa...  9.19 us
    all_to_all x1, waiting for transfers between devices, summed_on_arrival(): pieces = lax.all_to_all(cut_along(x, dim, length), axis, 0, 0, tiled=True)  8.89 us
  transfers between devices with their start and end apart: 5, of which 4 were waited for; matrix products, arithmetic and copies ran while one was open for 15% of the time, Pallas kernels for 0%

profile of v1, /device:TPU:1, one launch (start us, length us, event | category | flops | bytes accessed | tf_op | source)
XLA Modules:
  0.0 323.0 jit_solution(301139899295517346)
XLA Ops:
  8.0 0.0 copy-start
  8.0 0.0 all-gather.4.cloned.1.call-start
  8.1 0.7 all-gather.4.cloned.1.call-update
  8.7 0.0 all-gather.6.cloned.1.call-start
  8.8 2.2 fusion.26
  11.0 0.2 copy.28
  11.3 8.7 %reshape_squeeze.8 = bf16[208,2,13,8,16]{4,3,0,2,1:T(8,128)(2,1)} reshape(bf16[1,13,16,26,128]{4,2,1,3,0:T(8,128)(2,1)S(1)} %copy.28) | data formatting | bytes 2768896 | tf_op jit(solution)/shard_map/reshape;squeeze | solution.py:48
  20.0 10.9 %copy.29 = bf16[2,8,208,13,16]{2,4,3,1,0:T(8,128)(2,1)S(1)} copy(bf16[2,8,208,13,16]{4,1,2,3,0:T(8,128)(2,1)} %bitcast.62) | data formatting | bytes 2768896 | tf_op jit(solution)/shard_map/transpose | solution.py:51
  30.9 0.0 copy-done.6
  31.0 0.1 add.51
  31.1 32.3 %all-gather.4.cloned.1.call-done = bf16[16,208,1024]{2,1,0:T(8,128)(2,1)} async-done(((bf16[1,208,1024]{2,1,0:T(8,128)(2,1)}), bf16[16,208,1024]{2,1,0:T(8,128)(2,1)}) %all-gather.4.cloned.1.call-update) | async-done | bytes 6815760 | tf_op jit(solution)/shard_map/all_gather | solution.py:64
  63.3 4.6 %fusion.2 = f32[208,1024]{1,0:T(8,128)S(1)} fusion(bf16[16,208,208]{1,2,0:T(8,128)(2,1)S(1)} %bitcast.64, bf16[16,208,1024]{2,1,0:T(8,128)(2,1)} %all-gather.4.cloned.1.call-done, f32[208]{0:T(256)S(1)} %add.51), kind=kOutput, calls=%fused_computation.6 | convolution fusion | flops 1417887744 | bytes 9052992 | tf_op jit(solution)/shard_map/kib,koi->ob/dot_general | solution.py:58
  67.9 0.0 copy-done.1
  68.0 0.9 fusion.20
  68.8 0.0 all-gather.6.cloned.1.call-update
  68.9 0.2 copy.31
  69.1 8.7 %reshape_squeeze.9 = bf16[208,2,13,8,16]{4,3,0,2,1:T(8,128)(2,1)} reshape(bf16[1,13,16,26,128]{4,2,1,3,0:T(8,128)(2,1)S(1)} %copy.31) | data formatting | bytes 2768896 | tf_op jit(solution)/shard_map/reshape;squeeze | solution.py:48
  77.8 11.2 %copy.32 = bf16[2,8,208,13,16]{2,4,3,1,0:T(8,128)(2,1)S(1)} copy(bf16[2,8,208,13,16]{4,1,2,3,0:T(8,128)(2,1)} %bitcast.63) | data formatting | bytes 2768896 | tf_op jit(solution)/shard_map/transpose | solution.py:51
  89.0 0.0 copy-start.2
  89.0 0.1 add.55
  89.0 27.0 %all-gather.6.cloned.1.call-done = bf16[16,208,1024]{2,1,0:T(8,128)(2,1)} async-done(((bf16[1,208,1024]{2,1,0:T(8,128)(2,1)}), bf16[16,208,1024]{2,1,0:T(8,128)(2,1)}) %all-gather.6.cloned.1.call-update) | async-done | bytes 6815760 | tf_op jit(solution)/shard_map/all_gather | solution.py:64
  116.0 4.6 %fusion.3 = f32[1024,208]{0,1:T(8,128)S(1)} fusion(bf16[16,208,1024]{2,1,0:T(8,128)(2,1)} %all-gather.6.cloned.1.call-done, bf16[16,208,208]{1,2,0:T(8,128)(2,1)S(1)} %bitcast.71, f32[208]{0:T(256)S(1)} %add.55), kind=kOutput, calls=%fused_computation.7 | convolution fusion | flops 1417887744 | bytes 9052992 | tf_op jit(solution)/shard_map/kib,koi->ob/dot_general | solution.py:58
  120.6 0.0 copy-done.2
  120.6 0.2 fusion.19
  120.8 0.0 copy-start.3
  120.8 3.7 %stack.3 = bf16[16,1,208,1024]{3,2,1,0:T(8,128)(2,1)} broadcast(bf16[208,1024]{1,0:T(8,128)(2,1)S(1)} %bitcast.70), dimensions={2,3} | broadcast | bytes 7241728 | tf_op jit(solution)/shard_map/stack | solution.py:126
  124.5 0.0 copy-done.3
  124.5 4.9 %all-to-all-start = ((bf16[16,1,208,1024]{3,2,1,0:T(8,128)(2,1)}), bf16[16,1,208,1024]{3,2,1,0:T(8,128)(2,1)}, u32[]{:S(2)}, u32[]{:S(2)}) async-start(bf16[16,1,208,1024]{3,2,1,0:T(8,128)(2,1)} %stack.3), calls=%async_computation | async-start | bytes 13631488 | tf_op jit(solution)/shard_map/all_to_all | solution.py:125
  129.4 0.0 all-gather.8.cloned.1.call-start
  129.5 0.0 copy-done.5
  129.5 11.1 %all_gather.14 = bf16[1024,128]{1,0:T(8,128)(2,1)} all-gather(bf16[256,128]{1,0:T(8,128)(2,1)S(1)} %copy-done.5), channel_id=1, replica_groups=mesh['batch_0'=4,'batch_1'=4,'field'=2,'dim'=8] {'batch_1'}, dimensions={0}, use_global_device_ids=true | all-gather | bytes 327680 | tf_op jit(solution)/shard_map/all_gather | solution.py:15
  140.6 0.0 all-gather.8.cloned.1.call-update
  140.6 0.0 copy-done.4
  140.6 0.4 copy.34
  141.1 0.1 copy.35
  141.2 136.8 %all-to-all-done = bf16[16,1,208,1024]{3,2,1,0:T(8,128)(2,1)} async-done(((bf16[16,1,208,1024]{3,2,1,0:T(8,128)(2,1)}), bf16[16,1,208,1024]{3,2,1,0:T(8,128)(2,1)}, u32[]{:S(2)}, u32[]{:S(2)}) %all-to-all-start) | async-done | bytes 6815776 | tf_op jit(solution)/shard_map/all_to_all | solution.py:125
  278.0 0.0 copy-done
  278.0 5.2 %convolution_convert_fusion = bf16[1024,128]{1,0:T(8,128)(2,1)} fusion(bf16[64,128]{1,0:T(8,128)(2,1)S(1)} %copy-done, bf16[16,64,208]{1,2,0:T(8,128)(2,1)S(1)} %bitcast.68, bf16[16,1,208,1024]{3,2,1,0:T(8,128)(2,1)} %all-to-all-done, f32[64]{0:T(128)S(1)} %copy-done.7), kind=kOutput, calls=%fused_computation.8 | convolution fusion | flops 453312512 | bytes 7520512 | tf_op jit(solution)/shard_map/dot_general | solution.py:132
  283.2 6.7 %all-to-all-start.1 = ((bf16[16,64,128]{2,1,0:T(8,128)(2,1)}), bf16[16,64,128]{2,1,0:T(8,128)(2,1)S(1)}, u32[]{:S(2)}, u32[]{:S(2)}) async-start(bf16[16,64,128]{2,1,0:T(8,128)(2,1)} %bitcast.17), calls=%async_computation.1 | async-start | bytes 524288 | tf_op jit(solution)/shard_map/all_to_all | solution.py:27
  290.0 0.8 dynamic_slice.7
  290.7 8.9 %all-to-all-done.1 = bf16[16,64,128]{2,1,0:T(8,128)(2,1)S(1)} async-done(((bf16[16,64,128]{2,1,0:T(8,128)(2,1)}), bf16[16,64,128]{2,1,0:T(8,128)(2,1)S(1)}, u32[]{:S(2)}, u32[]{:S(2)}) %all-to-all-start.1) | async-done | bytes 262176 | tf_op jit(solution)/shard_map/all_to_all | solution.py:27
  299.7 0.0 all-gather.8.cloned.1.call-done
  299.7 1.8 fusion.27
  301.5 0.5 exponential_reduce_fusion
  302.0 11.7 %all_to_all.16 = f32[16,1,64]{2,1,0:T(1,128)S(1)} all-to-all(f32[16,1,64]{2,1,0:T(1,128)S(1)} %broadcast_in_dim.15), channel_id=1, replica_groups=mesh['batch_0'=4,'batch_1'=4,'field'=2,'dim'=8] {'field','dim'}, dimensions={0} | all-to-all | bytes 8192 | tf_op jit(solution)/shard_map/all_to_all | solution.py:39
  313.7 0.5 broadcast.20
  314.3 0.7 reduce.7
  314.9 0.7 reshape.68
  (11 shorter events, 0.1 us)
Async XLA Ops:
  8.0 270.0 %copy-start = (bf16[64,128]{1,0:T(8,128)(2,1)S(1)}, bf16[64,128]{1,0:T(8,128)(2,1)}, u32[]{:S(2)}) copy-start(bf16[64,128]{1,0:T(8,128)(2,1)} %param.14) | copy-start | bytes 49156
  8.0 55.3 %all-gather.4.cloned.1.call-start = ((), (), s32[]{:S(2)}) async-start(), calls=%async_computation.3 | async-start | bytes 7241728 | tf_op jit(solution)/shard_map/all_gather | solution.py:64
  8.7 107.3 %all-gather.6.cloned.1.call-start = ((), (), s32[]{:S(2)}) async-start(), calls=%async_computation.4 | async-start | bytes 7241728 | tf_op jit(solution)/shard_map/all_gather | solution.py:64
  20.0 11.0 %copy-start.6 = (f32[2,13,16]{2,0,1:T(2,128)S(1)}, f32[2,13,16]{2,0,1:T(2,128)}, u32[]{:S(2)}) copy-start(f32[2,13,16]{2,0,1:T(2,128)} %param.11) | copy-start | bytes 4996
  63.3 4.6 %copy-start.1 = (bf16[13,16,1024]{2,1,0:T(8,128)(2,1)S(1)}, bf16[13,16,1024]{2,1,0:T(8,128)(2,1)}, u32[]{:S(2)}) copy-start(bf16[13,16,1024]{2,1,0:T(8,128)(2,1)} %param.9) | copy-start | bytes 1277956
  89.0 31.6 %copy-start.2 = (bf16[13,16,1024]{2,1,0:T(8,128)(2,1)S(1)}, bf16[13,16,1024]{2,1,0:T(8,128)(2,1)}, u32[]{:S(2)}) copy-start(bf16[13,16,1024]{2,1,0:T(8,128)(2,1)} %fusion.20) | copy-start | bytes 1277956
  120.8 3.7 %copy-start.3 = (bf16[13,16,1024]{2,1,0:T(8,128)(2,1)}, bf16[13,16,1024]{2,1,0:T(8,128)(2,1)S(1)}, u32[]{:S(2)}) copy-start(bf16[13,16,1024]{2,1,0:T(8,128)(2,1)S(1)} %fusion.19) | copy-start | bytes 1277956
  124.5 4.9 %copy-start.5 = (bf16[256,128]{1,0:T(8,128)(2,1)S(1)}, bf16[256,128]{1,0:T(8,128)(2,1)}, u32[]{:S(2)}) copy-start(bf16[256,128]{1,0:T(8,128)(2,1)} %param.16) | copy-start | bytes 196612
  124.5 16.1 %copy-start.4 = (bf16[64,26,128]{2,0,1:T(8,128)(2,1)S(1)}, bf16[64,26,128]{2,0,1:T(8,128)(2,1)}, u32[]{:S(2)}) copy-start(bf16[64,26,128]{2,0,1:T(8,128)(2,1)} %param.12) | copy-start | bytes 1277956
  124.5 153.5 %copy-start.7 = (f32[64]{0:T(128)S(1)}, f32[64]{0:T(128)}, u32[]{:S(2)}) copy-start(f32[64]{0:T(128)} %param.13) | copy-start | bytes 772
  124.5 153.5 %all-to-all-start = ((bf16[16,1,208,1024]{3,2,1,0:T(8,128)(2,1)}), bf16[16,1,208,1024]{3,2,1,0:T(8,128)(2,1)}, u32[]{:S(2)}, u32[]{:S(2)}) async-start(bf16[16,1,208,1024]{3,2,1,0:T(8,128)(2,1)} %stack.3), calls=%async_computation | async-start | bytes 13631488 | tf_op jit(solution)/shard_map/all_to_all | solution.py:125
  129.4 170.3 %all-gather.8.cloned.1.call-start = ((), (), s32[]{:S(2)}) async-start(), calls=%async_computation.5 | async-start | bytes 1310720 | tf_op jit(solution)/shard_map/all_gather | solution.py:15
  283.2 16.4 %all-to-all-start.1 = ((bf16[16,64,128]{2,1,0:T(8,128)(2,1)}), bf16[16,64,128]{2,1,0:T(8,128)(2,1)S(1)}, u32[]{:S(2)}, u32[]{:S(2)}) async-start(bf16[16,64,128]{2,1,0:T(8,128)(2,1)} %bitcast.17), calls=%async_computation.1 | async-start | bytes 524288 | tf_op jit(solution)/shard_map/all_to_all | solution.py:27
Sparse Core Ops, SparseCore 0:
  10.6 52.6 all-gather.3
  69.0 46.9 all-gather.5
Sparse Core Ops, SparseCore 1:
  140.7 27.1 all-gather.7
